TPU v7x, 32 devices: a whole 2x2x4 slice. The times are simulated.
32 devices in a mesh: heads: 4 (over x, core), ctx: 8 (over z, y).
Axes of the slice: x: 2, y: 2, z: 4, core: 2. Of those that a mesh axis runs over, the one named last changes fastest.
Arguments:
- queries: bfloat16 [1536, 2048], P('ctx', 'heads'), may hold values from -6 to 6
- key_states: bfloat16 [1536, 512], P('ctx', 'heads'), may hold values from -6 to 6
- value_states: bfloat16 [1536, 512], P('ctx', 'heads'), may hold values from -6 to 6
- attention_out: bfloat16 [1536, 2048], P('ctx', 'heads'), may hold values from -2 to 2
- out_grad: bfloat16 [1536, 2048], P('ctx', 'heads'), may hold values from -6 to 6
- log_sum_exp: float32 [16, 1536], P('heads', 'ctx'), may hold values from 0 to 16, as said below
- block_counts: int32 [8], replicated, may hold values from 1 to 3, as said below
- w_query: bfloat16 [4096, 2048], P(None, 'heads'), may hold values from -0.09375 to 0.09375
- w_key: bfloat16 [4096, 512], P(None, 'heads'), may hold values from -0.09375 to 0.09375
- w_value: bfloat16 [4096, 512], P(None, 'heads'), may hold values from -0.09375 to 0.09375
Outputs:
- input_grad: bfloat16 [1536, 4096], P('ctx', 'heads')
- key_grad: float32 [1536, 512], P('ctx', 'heads')
- value_grad: float32 [1536, 512], P('ctx', 'heads')
Inputs may be any that keep to these rules, and one draw needn't show every extreme that they name: `block_counts`: one entry equals 3. `log_sum_exp`: finite offsets of each row's scores.
All inputs are finite; a program needn't handle non-finite values.
Results may differ from a plain program's by a relative error of at most 0.0063.
Values may be sent and summed in bfloat16 or wider, within the bound.
A program may use at most 128 MiB of HBM per device.

v0:
```python
import math
import jax
import jax.numpy as jnp
from jax import lax
from jax.sharding import PartitionSpec as P

BLOCK = 64


def key_span(row_count, capacity):
    shards = row_count // capacity
    per_step = max(1, min(shards, 512 // capacity))
    while shards % per_step:
        per_step = per_step - 1
    return per_step * capacity


def row_info(row_index, lengths, offsets, capacity):
    device = row_index // capacity
    onehot = device[:, None] == jnp.arange(lengths.shape[0], dtype=jnp.int32)[None, :]
    length = jnp.sum(jnp.where(onehot, lengths[None, :], 0), axis=1)
    offset = jnp.sum(jnp.where(onehot, offsets[None, :], 0), axis=1)
    within = row_index - device * capacity
    return (offset + within, within < length)


def tile_grads(
    query_blk,
    grad_blk,
    norm_blk,
    delta_blk,
    query_pos,
    query_live,
    key_blk,
    value_blk,
    key_pos,
    key_live,
    score_scale,
):
    scores = (
        jnp.einsum("qgd,kd->gqk", query_blk, key_blk, preferred_element_type=jnp.float32)
        * score_scale
    )
    visible = query_live[:, None] & key_live[None, :] & (key_pos[None, :] <= query_pos[:, None])
    probability = jnp.where(visible[None], jnp.exp(scores - norm_blk.T[:, :, None]), 0.0)
    prob_grad = jnp.einsum("qgd,kd->gqk", grad_blk, value_blk, preferred_element_type=jnp.float32)
    score_grad = probability * (prob_grad - delta_blk.T[:, :, None])
    return (probability.astype(jnp.bfloat16), score_grad.astype(jnp.bfloat16))


def on_device(
    queries,
    key_states,
    value_states,
    attention_out,
    out_grad,
    log_sum_exp,
    block_counts,
    w_query,
    w_key,
    w_value,
):
    capacity = key_states.shape[0]
    head_dim = key_states.shape[1]
    group = queries.shape[1] // head_dim
    score_scale = 1.0 / math.sqrt(head_dim)
    own_index = lax.axis_index("ctx")
    lengths = block_counts * BLOCK
    offsets = jnp.cumsum(lengths) - lengths
    own_rows = own_index * capacity + jnp.arange(capacity, dtype=jnp.int32)
    own_pos, own_live = row_info(own_rows, lengths, offsets, capacity)
    query_heads = queries.reshape(capacity, group, head_dim)
    grad_heads = out_grad.reshape(capacity, group, head_dim)
    output_heads = attention_out.reshape(capacity, group, head_dim)
    delta_rows = jnp.sum(grad_heads.astype(jnp.float32) * output_heads.astype(jnp.float32), axis=2)
    norm_rows = log_sum_exp.T
    zero_rows = jnp.zeros((capacity, group, head_dim), jnp.float32)
    zero_own = jnp.zeros((capacity, head_dim), jnp.float32)
    key_piece = lax.all_gather(key_states, "ctx", axis=0, tiled=True)
    value_piece = lax.all_gather(value_states, "ctx", axis=0, tiled=True)
    span = key_span(key_piece.shape[0], capacity)

    def step(block_num, query_grad):
        begin_row = block_num * span
        key_blk = lax.dynamic_slice_in_dim(key_piece, begin_row, span, 0)
        value_blk = lax.dynamic_slice_in_dim(value_piece, begin_row, span, 0)
        key_pos, key_live = row_info(
            begin_row + jnp.arange(span, dtype=jnp.int32), lengths, offsets, capacity
        )

        def compute():
            prob_b, grad_b = tile_grads(
                query_heads,
                grad_heads,
                norm_rows,
                delta_rows,
                own_pos,
                own_live,
                key_blk,
                value_blk,
                key_pos,
                key_live,
                score_scale,
            )
            return score_scale * jnp.einsum(
                "gqk,kd->qgd", grad_b, key_blk, preferred_element_type=jnp.float32
            )

        terms = compute()
        return query_grad + terms

    query_grad = lax.fori_loop(0, key_piece.shape[0] // span, step, zero_rows)
    norm_all, delta_all = (
        lax.all_gather(norm_rows, "ctx", axis=0, tiled=True),
        lax.all_gather(delta_rows, "ctx", axis=0, tiled=True),
    )
    query_piece = lax.all_gather(queries, "ctx", axis=0, tiled=True)
    grad_piece = lax.all_gather(out_grad, "ctx", axis=0, tiled=True)
    fold_span = key_span(query_piece.shape[0], capacity)

    def step(block_num, state):
        key_acc, value_acc = state
        begin_row = block_num * fold_span
        query_blk = lax.dynamic_slice_in_dim(query_piece, begin_row, fold_span, 0).reshape(
            fold_span, group, head_dim
        )
        grad_blk = lax.dynamic_slice_in_dim(grad_piece, begin_row, fold_span, 0).reshape(
            fold_span, group, head_dim
        )
        norm_blk = lax.dynamic_slice_in_dim(norm_all, begin_row, fold_span, 0)
        delta_blk = lax.dynamic_slice_in_dim(delta_all, begin_row, fold_span, 0)
        query_pos, query_live = row_info(
            begin_row + jnp.arange(fold_span, dtype=jnp.int32), lengths, offsets, capacity
        )

        def compute():
            prob_b, grad_b = tile_grads(
                query_blk,
                grad_blk,
                norm_blk,
                delta_blk,
                query_pos,
                query_live,
                key_states,
                value_states,
                own_pos,
                own_live,
                score_scale,
            )
            return (
                score_scale
                * jnp.einsum("gqk,qgd->kd", grad_b, query_blk, preferred_element_type=jnp.float32),
                jnp.einsum("gqk,qgd->kd", prob_b, grad_blk, preferred_element_type=jnp.float32),
            )

        terms = compute()
        return (key_acc + terms[0], value_acc + terms[1])

    key_grad, value_grad = lax.fori_loop(
        0, query_piece.shape[0] // fold_span, step, (zero_own, zero_own)
    )
    query_flat = query_grad.reshape(capacity, group * head_dim).astype(jnp.bfloat16)
    partial_input = jnp.einsum("rc,mc->rm", query_flat, w_query, preferred_element_type=jnp.float32)
    partial_input = partial_input + jnp.einsum(
        "rc,mc->rm", key_grad.astype(jnp.bfloat16), w_key, preferred_element_type=jnp.float32
    )
    partial_input = partial_input + jnp.einsum(
        "rc,mc->rm", value_grad.astype(jnp.bfloat16), w_value, preferred_element_type=jnp.float32
    )
    input_part = lax.psum_scatter(partial_input, "heads", scatter_dimension=1, tiled=True)
    return (input_part.astype(jnp.bfloat16), key_grad, value_grad)


def solution(mesh):
    return jax.shard_map(
        on_device,
        mesh=mesh,
        in_specs=(
            P("ctx", "heads"),
            P("ctx", "heads"),
            P("ctx", "heads"),
            P("ctx", "heads"),
            P("ctx", "heads"),
            P("heads", "ctx"),
            P(),
            P(None, "heads"),
            P(None, "heads"),
            P(None, "heads"),
        ),
        out_specs=(P("ctx", "heads"), P("ctx", "heads"), P("ctx", "heads")),
        check_vma=False,
    )
```

profile of v0, /device:TPU:0, one launch (start us, length us, event | category | flops | bytes accessed | tf_op | source)
XLA Modules:
  0.0 253.6 jit_solution(5064324992087366843)
XLA Ops:
  15.1 34.2 %all_gather.18 = bf16[1536,128]{1,0:T(8,128)(2,1)S(1)} all-gather(bf16[192,128]{1,0:T(8,128)(2,1)} %param.15), channel_id=1, replica_groups=mesh['heads'=4,'ctx'=8] {'ctx'}, dimensions={0}, use_global_device_ids=true | all-gather | bytes 442368 | tf_op jit(solution)/shard_map/all_gather | solution.py:79
  49.3 33.4 %all_gather.19 = bf16[1536,128]{1,0:T(8,128)(2,1)} all-gather(bf16[192,128]{1,0:T(8,128)(2,1)S(1)} %copy-done.3), channel_id=1, replica_groups=mesh['heads'=4,'ctx'=8] {'ctx'}, dimensions={0}, use_global_device_ids=true | all-gather | bytes 442368 | tf_op jit(solution)/shard_map/all_gather | solution.py:80
  82.7 18.1 %while.34 = (s32[]{:T(128)}, f32[192,4,128]{2,0,1:T(8,128)S(1)}, bf16[1536,128]{1,0:T(8,128)(2,1)S(1)}, pred[192]{0:T(512)(128)(4,1)}, s32[8]{0:T(128)}, /*index...) while((s32[]{:T(128)}, f32[192,4,128]{2,0,1:T(8,128)S(1)}, ...), condition=%wide.region_7.8_spmd.clone, body=%wide.region_4.7_spmd.clone.sunk | while | flops 228805248 | bytes 4005340 | solution.py:112
  84.3 1.4 fusion.93
  85.7 1.5 fusion.94
  88.8 1.4 fusion.93
  90.2 1.5 fusion.94
  93.4 1.4 fusion.93
  94.7 1.5 fusion.94
  97.9 1.4 fusion.93
  99.3 1.5 fusion.94
  100.9 30.6 %all-gather.1 = f32[8,192,4]{1,2,0:T(4,128)S(1)} all-gather(f32[1,192,4]{1,2,0:T(4,128)S(1)} %copy.55), channel_id=1, replica_groups=mesh['heads'=4,'ctx'=8] {'ctx'}, dimensions={0}, use_global_device_ids=true | all-gather | bytes 27648 | tf_op jit(solution)/shard_map/all_gather | solution.py:115
  132.3 30.6 %all-gather = f32[8,192,4]{1,2,0:T(4,128)S(1)} all-gather(f32[1,192,4]{1,2,0:T(4,128)S(1)} %bitcast.173), channel_id=1, replica_groups=mesh['heads'=4,'ctx'=8] {'ctx'}, dimensions={0}, use_global_device_ids=true | all-gather | bytes 27648 | tf_op jit(solution)/shard_map/all_gather | solution.py:114
  163.6 5.4 %fusion.46 = f32[192,4096]{1,0:T(8,128)} fusion(bf16[4096,512]{1,0:T(8,128)(2,1)} %param.21, f32[192,4,128]{2,0,1:T(8,128)S(1)} %get-tuple-element.600), kind=kOutput, calls=%fused_computation.72 | convolution fusion | flops 805404672 | bytes 7733248 | tf_op jit(solution)/shard_map/rc,mc->rm/dot_general | solution.py:163
  168.9 31.9 %while.35 = (s32[]{:T(128)}, f32[192,128]{1,0:T(8,128)S(1)}, f32[192,128]{1,0:T(8,128)}, s32[8]{0:T(128)}, pred[192]{0:T(512)(128)(4,1)}, /*index=5*/s32[192]{0:...) while((s32[]{:T(128)}, f32[192,128]{1,0:T(8,128)S(1)}, ...), condition=%wide.region_11.12_spmd.clone, body=%wide.region_8.11_spmd.clone.sunk | while | flops 304425600 | bytes 8972294 | solution.py:159
  171.9 1.3 dynamic-slice_bitcast_fusion.3
  182.0 1.9 fusion.106
  187.4 1.3 dynamic-slice_bitcast_fusion.3
  190.2 1.9 fusion.106
  198.4 1.9 fusion.106
  200.9 2.6 %convolution_add_fusion.1 = f32[192,4096]{1,0:T(8,128)S(1)} fusion(f32[192,4096]{1,0:T(8,128)} %fusion.46, bf16[4096,128]{1,0:T(8,128)(2,1)S(1)} %copy-done, f32[192,128]{1,0:T(8,128)S(1)} %get-tuple-element.598), kind=kOutput, calls=%fused_computation.70 | convolution fusion | flops 202137600 | bytes 7438336 | tf_op jit(solution)/shard_map/rc,mc->rm/dot_general | solution.py:164
  203.5 2.2 convolution_add_fusion
  205.8 39.4 %reduce-scatter.2.cloned.1.call-done = f32[192,1024]{1,0:T(8,128)} async-done(((f32[192,4096]{1,0:T(8,128)}), f32[192,1024]{1,0:T(8,128)}) %reduce-scatter.2.cloned.1.call-update) | async-done | bytes 786448 | tf_op jit(solution)/shard_map/reduce_scatter | solution.py:170
  245.1 1.9 convert_element_type.61
  (118 shorter events, 39.0 us)
Async XLA Ops:
  7.2 193.7 %copy-start = (bf16[4096,128]{1,0:T(8,128)(2,1)S(1)}, bf16[4096,128]{1,0:T(8,128)(2,1)}, u32[]{:S(2)}) copy-start(bf16[4096,128]{1,0:T(8,128)(2,1)} %param.22) | copy-start | bytes 3145732
  7.2 3.5 %copy-start.5 = (bf16[192,512]{1,0:T(8,128)(2,1)S(1)}, bf16[192,512]{1,0:T(8,128)(2,1)}, u32[]{:S(2)}) copy-start(bf16[192,512]{1,0:T(8,128)(2,1)} %param.14) | copy-start | bytes 589828
  7.2 4.2 %copy-start.9 = (s32[8]{0:T(128)S(1)}, s32[8]{0:T(128)}, u32[]{:S(2)}) copy-start(s32[8]{0:T(128)} %param.20) | copy-start | bytes 100
  7.2 7.4 %copy-start.7 = (bf16[192,512]{1,0:T(8,128)(2,1)S(1)}, bf16[192,512]{1,0:T(8,128)(2,1)}, u32[]{:S(2)}) copy-start(bf16[192,512]{1,0:T(8,128)(2,1)} %param.17) | copy-start | bytes 589828
  7.2 161.7 %all-gather.5.cloned.1.call-start = ((), (), s32[]{:S(2)}) async-start(), calls=%async_computation.1 | async-start | bytes 1769472 | tf_op jit(solution)/shard_map/all_gather | solution.py:117
  7.9 161.0 %all-gather.7.cloned.1.call-start = ((), (), s32[]{:S(2)}) async-start(), calls=%async_computation.2 | async-start | bytes 1769472 | tf_op jit(solution)/shard_map/all_gather | solution.py:118
  8.7 236.4 %reduce-scatter.2.cloned.1.call-start = ((), (), s32[]{:S(2)}) async-start(), calls=%async_computation.3 | async-start | bytes 3932160 | tf_op jit(solution)/shard_map/reduce_scatter | solution.py:170
  10.7 38.6 %copy-start.3 = (bf16[192,128]{1,0:T(8,128)(2,1)S(1)}, bf16[192,128]{1,0:T(8,128)(2,1)}, u32[]{:S(2)}) copy-start(bf16[192,128]{1,0:T(8,128)(2,1)} %param.16) | copy-start | bytes 147460
  11.4 71.3 %copy-start.8 = (f32[4,192]{1,0:T(4,128)S(1)}, f32[4,192]{1,0:T(4,128)}, u32[]{:S(2)}) copy-start(f32[4,192]{1,0:T(4,128)} %param.19) | copy-start | bytes 9220
  174.6 1.0 copy-start.6
  181.9 1.9 copy-start.6
  190.2 1.9 copy-start.6
  198.4 1.9 copy-start.6
  200.9 2.6 %copy-start.1 = (f32[192,128]{1,0:T(8,128)}, f32[192,128]{1,0:T(8,128)S(1)}, u32[]{:S(2)}) copy-start(f32[192,128]{1,0:T(8,128)S(1)} %get-tuple-element.598) | copy-start | bytes 294916
  200.9 2.6 %copy-start.2 = (f32[192,128]{1,0:T(8,128)S(1)}, f32[192,128]{1,0:T(8,128)}, u32[]{:S(2)}) copy-start(f32[192,128]{1,0:T(8,128)} %get-tuple-element.599) | copy-start | bytes 294916
  200.9 2.6 %copy-start.4 = (bf16[4096,128]{1,0:T(8,128)(2,1)S(1)}, bf16[4096,128]{1,0:T(8,128)(2,1)}, u32[]{:S(2)}) copy-start(bf16[4096,128]{1,0:T(8,128)(2,1)} %param.23) | copy-start | bytes 3145732
Sparse Core Ops, SparseCore 0:
  10.2 50.6 all-gather.4
  63.1 43.6 all-gather.6
  205.9 39.1 reduce-scatter.1
where the time goes:
time: 255 us; the launch traced here: 254 us
  blocking collectives  129 us (51%)
  waiting for transfers between devices  40.8 us (16%)
  matrix products  35.5 us (14%)
  other arithmetic  18 us (7%)
  local copies, waits for them, and re-layouts  16 us (6%)
  between operations  13.9 us (5%)
    reduce_scatter x1, waiting for transfers between devices, on_device(): lax.psum_scatter(partial_input, 'heads', scatter_dimension=1, tiled=True)  39.4 us
    all_gather x1, blocking collectives, on_device(): key_piece = lax.all_gather(key_states, 'ctx', axis=0, tiled=True)  34.2 us
    all_gather x1, blocking collectives, on_device(): value_piece = lax.all_gather(value_states, 'ctx', axis=0, tiled=True)  33.4 us
    all_gather x1, blocking collectives, on_device(): lax.all_gather(delta_rows, 'ctx', axis=0, tiled=True)  30.6 us
    all_gather x1, blocking collectives, on_device(): lax.all_gather(norm_rows, 'ctx', axis=0, tiled=True)  30.6 us
    dot_general x8, matrix products, tile_grads(): jnp.einsum('qgd,kd->gqk', query_blk, key_blk, preferred_element_type=jnp....  10.2 us
    dot_general x4, matrix products, compute(): jnp.einsum('gqk,qgd->kd', prob_b, grad_blk, preferred_element_type=jnp.fl...  6.56 us
    and x8, other arithmetic, tile_grads(): query_live[:, None] & key_live[None, :]  6.44 us
  transfers between devices with their start and end apart: 3, of which 1 were waited for; matrix products, arithmetic and copies ran while one was open for 12% of the time, Pallas kernels for 0%

commit v1 on v0

--- a/solution.py
+++ b/solution.py
@@ -76,7 +76,16 @@
     norm_rows = log_sum_exp.T
     zero_rows = jnp.zeros((capacity, group, head_dim), jnp.float32)
     zero_own = jnp.zeros((capacity, head_dim), jnp.float32)
-    key_piece = lax.all_gather(key_states, "ctx", axis=0, tiled=True)
+    deliver_patch = lambda m, dimension_no: jnp.concatenate(
+        jax.lax.all_to_all(
+            jnp.stack([m for _ in range(jax.lax.psum(1, axis_name="ctx"))], 0),
+            axis_name="ctx",
+            split_axis=0,
+            concat_axis=0,
+        ),
+        dimension_no,
+    )
+    key_piece = deliver_patch(key_states, 0)
     value_piece = lax.all_gather(value_states, "ctx", axis=0, tiled=True)
     span = key_span(key_piece.shape[0], capacity)
 

time: 255 us -> 229 us (0.90)
  blocking collectives: 129 us -> 98.3 us
  starting transfers between devices: 0.11 us -> 7.43 us
    all_gather x1 -> x0, blocking collectives: 34.2 us -> none  [on_device(): key_piece = lax.all_gather(key_states, 'ctx', axis=0, tiled=True)]
    all_to_all x0 -> x1, starting transfers between devices: none -> 7.31 us  [on_device(): jax.lax.all_to_all(jnp.stack([m for _ in range(jax.lax.psum(1, axis_name=...]
    all_gather x1, blocking collectives: 30.6 us -> 33.7 us  [on_device(): lax.all_gather(delta_rows, 'ctx', axis=0, tiled=True)]
  transfers between devices with their start and end apart: 3 -> 4, of which waited for: 1 -> 1; matrix products, arithmetic and copies ran while one was open for 12% -> 14% of each run, Pallas kernels for 0% -> 0%
where the time goes in v1:
time: 229 us; the launch traced here: 228 us
  blocking collectives  98.3 us (43%)
  waiting for transfers between devices  38.3 us (17%)
  matrix products  35.4 us (15%)
  other arithmetic  17.7 us (8%)
  local copies, waits for them, and re-layouts  16.3 us (7%)
  between operations  13.9 us (6%)
  starting transfers between devices  7.43 us (3%)
    reduce_scatter x1, waiting for transfers between devices, on_device(): lax.psum_scatter(partial_input, 'heads', scatter_dimension=1, tiled=True)  36.9 us
    all_gather x1, blocking collectives, on_device(): value_piece = lax.all_gather(value_states, 'ctx', axis=0, tiled=True)  33.8 us
    all_gather x1, blocking collectives, on_device(): lax.all_gather(delta_rows, 'ctx', axis=0, tiled=True)  33.7 us
    all_gather x1, blocking collectives, on_device(): lax.all_gather(norm_rows, 'ctx', axis=0, tiled=True)  30.7 us
    dot_general x8, matrix products, tile_grads(): jnp.einsum('qgd,kd->gqk', query_blk, key_blk, preferred_element_type=jnp....  10.2 us
    all_to_all x1, starting transfers between devices, on_device(): jax.lax.all_to_all(jnp.stack([m for _ in range(jax.lax.psum(1, axis_name=...  7.31 us
    dot_general x4, matrix products, compute(): jnp.einsum('gqk,qgd->kd', prob_b, grad_blk, preferred_element_type=jnp.fl...  6.56 us
    and x8, other arithmetic, tile_grads(): query_live[:, None] & key_live[None, :]  6.34 us
  transfers between devices with their start and end apart: 4, of which 1 were waited for; matrix products, arithmetic and copies ran while one was open for 14% of the time, Pallas kernels for 0%

profile of v1, /device:TPU:0, one launch (start us, length us, event | category | flops | bytes accessed | tf_op | source)
XLA Modules:
  0.0 228.0 jit_solution(17212041036027023935)
XLA Ops:
  7.9 1.6 stack.2
  9.5 7.3 %all-to-all-start = ((bf16[8,192,128]{2,1,0:T(8,128)(2,1)}), bf16[8,192,128]{2,1,0:T(8,128)(2,1)S(1)}, u32[]{:S(2)}, u32[]{:S(2)}) async-start(bf16[8,192,128]{2,1,0:T(8,128)(2,1)} %stack.2), calls=%async_computation | async-start | bytes 786432 | tf_op jit(solution)/shard_map/all_to_all | solution.py:80
  21.4 33.7 %all-gather.1 = f32[8,192,4]{1,2,0:T(4,128)S(1)} all-gather(f32[1,192,4]{1,2,0:T(4,128)S(1)} %copy.55), channel_id=1, replica_groups=mesh['heads'=4,'ctx'=8] {'ctx'}, dimensions={0}, use_global_device_ids=true | all-gather | bytes 27648 | tf_op jit(solution)/shard_map/all_gather | solution.py:124
  55.8 30.7 %all-gather = f32[8,192,4]{1,2,0:T(4,128)S(1)} all-gather(f32[1,192,4]{1,2,0:T(4,128)} %bitcast.4), channel_id=1, replica_groups=mesh['heads'=4,'ctx'=8] {'ctx'}, dimensions={0}, use_global_device_ids=true | all-gather | bytes 27648 | tf_op jit(solution)/shard_map/all_gather | solution.py:123
  87.3 33.8 %all_gather.15 = bf16[1536,128]{1,0:T(8,128)(2,1)} all-gather(bf16[192,128]{1,0:T(8,128)(2,1)S(1)} %copy-done.4), channel_id=1, replica_groups=mesh['heads'=4,'ctx'=8] {'ctx'}, dimensions={0}, use_global_device_ids=true | all-gather | bytes 442368 | tf_op jit(solution)/shard_map/all_gather | solution.py:89
  122.4 18.1 %while.34 = (s32[]{:T(128)}, f32[192,4,128]{2,0,1:T(8,128)S(1)}, bf16[1536,128]{1,0:T(8,128)(2,1)S(1)}, pred[192]{0:T(512)(128)(4,1)}, s32[8]{0:T(128)}, /*index...) while((s32[]{:T(128)}, f32[192,4,128]{2,0,1:T(8,128)S(1)}, ...), condition=%wide.region_7.8_spmd.clone, body=%wide.region_4.7_spmd.clone.sunk | while | flops 228805248 | bytes 4016632 | solution.py:121
  124.0 1.4 fusion.93
  125.4 1.5 fusion.94
  128.5 1.4 fusion.93
  129.9 1.5 fusion.94
  133.1 1.4 fusion.93
  134.4 1.5 fusion.94
  137.6 1.4 fusion.93
  139.0 1.5 fusion.94
  140.5 5.4 %fusion.46 = f32[192,4096]{1,0:T(8,128)} fusion(bf16[4096,512]{1,0:T(8,128)(2,1)} %param.21, f32[192,4,128]{2,0,1:T(8,128)S(1)} %get-tuple-element.600), kind=kOutput, calls=%fused_computation.72 | convolution fusion | flops 805404672 | bytes 7733248 | tf_op jit(solution)/shard_map/rc,mc->rm/dot_general | solution.py:172
  145.9 31.9 %while.35 = (s32[]{:T(128)}, f32[192,128]{1,0:T(8,128)S(1)}, f32[192,128]{1,0:T(8,128)}, s32[8]{0:T(128)}, pred[192]{0:T(512)(128)(4,1)}, /*index=5*/s32[192]{0:...) while((s32[]{:T(128)}, f32[192,128]{1,0:T(8,128)S(1)}, ...), condition=%wide.region_11.12_spmd.clone, body=%wide.region_8.11_spmd.clone.sunk | while | flops 304425600 | bytes 8972294 | solution.py:168
  148.9 1.3 dynamic-slice_bitcast_fusion.3
  158.9 1.9 fusion.106
  167.1 1.9 fusion.106
  175.3 1.9 fusion.106
  177.8 2.6 %convolution_add_fusion.1 = f32[192,4096]{1,0:T(8,128)S(1)} fusion(f32[192,4096]{1,0:T(8,128)} %fusion.46, bf16[4096,128]{1,0:T(8,128)(2,1)S(1)} %copy-done, f32[192,128]{1,0:T(8,128)S(1)} %get-tuple-element.598), kind=kOutput, calls=%fused_computation.70 | convolution fusion | flops 202137600 | bytes 7438336 | tf_op jit(solution)/shard_map/rc,mc->rm/dot_general | solution.py:173
  180.4 2.2 convolution_add_fusion
  182.7 36.9 %reduce-scatter.2.cloned.1.call-done = f32[192,1024]{1,0:T(8,128)} async-done(((f32[192,4096]{1,0:T(8,128)}), f32[192,1024]{1,0:T(8,128)}) %reduce-scatter.2.cloned.1.call-update) | async-done | bytes 786448 | tf_op jit(solution)/shard_map/reduce_scatter | solution.py:179
  219.5 1.9 convert_element_type.61
  (128 shorter events, 38.8 us)
Async XLA Ops:
  7.2 170.6 %copy-start = (bf16[4096,128]{1,0:T(8,128)(2,1)S(1)}, bf16[4096,128]{1,0:T(8,128)(2,1)}, u32[]{:S(2)}) copy-start(bf16[4096,128]{1,0:T(8,128)(2,1)} %param.22) | copy-start | bytes 3145732
  7.2 10.5 %copy-start.3 = (bf16[192,512]{1,0:T(8,128)(2,1)S(1)}, bf16[192,512]{1,0:T(8,128)(2,1)}, u32[]{:S(2)}) copy-start(bf16[192,512]{1,0:T(8,128)(2,1)} %param.18) | copy-start | bytes 589828
  7.2 10.6 %copy-start.10 = (s32[8]{0:T(128)S(1)}, s32[8]{0:T(128)}, u32[]{:S(2)}) copy-start(s32[8]{0:T(128)} %param.20) | copy-start | bytes 100
  7.2 13.1 %copy-start.8 = (bf16[192,512]{1,0:T(8,128)(2,1)S(1)}, bf16[192,512]{1,0:T(8,128)(2,1)}, u32[]{:S(2)}) copy-start(bf16[192,512]{1,0:T(8,128)(2,1)} %param.17) | copy-start | bytes 589828
  7.2 138.7 %all-gather.5.cloned.1.call-start = ((), (), s32[]{:S(2)}) async-start(), calls=%async_computation.2 | async-start | bytes 1769472 | tf_op jit(solution)/shard_map/all_gather | solution.py:126
  9.5 112.9 %all-to-all-start = ((bf16[8,192,128]{2,1,0:T(8,128)(2,1)}), bf16[8,192,128]{2,1,0:T(8,128)(2,1)S(1)}, u32[]{:S(2)}, u32[]{:S(2)}) async-start(bf16[8,192,128]{2,1,0:T(8,128)(2,1)} %stack.2), calls=%async_computation | async-start | bytes 786432 | tf_op jit(solution)/shard_map/all_to_all | solution.py:80
  16.9 70.4 %copy-start.4 = (bf16[192,128]{1,0:T(8,128)(2,1)S(1)}, bf16[192,128]{1,0:T(8,128)(2,1)}, u32[]{:S(2)}) copy-start(bf16[192,128]{1,0:T(8,128)(2,1)} %param.16) | copy-start | bytes 147460
  16.9 129.0 %all-gather.7.cloned.1.call-start = ((), (), s32[]{:S(2)}) async-start(), calls=%async_computation.3 | async-start | bytes 1769472 | tf_op jit(solution)/shard_map/all_gather | solution.py:127
  17.6 201.9 %reduce-scatter.2.cloned.1.call-start = ((), (), s32[]{:S(2)}) async-start(), calls=%async_computation.4 | async-start | bytes 3932160 | tf_op jit(solution)/shard_map/reduce_scatter | solution.py:179
  20.3 101.4 %copy-start.6 = (bf16[192,512]{1,0:T(8,128)(2,1)S(1)}, bf16[192,512]{1,0:T(8,128)(2,1)}, u32[]{:S(2)}) copy-start(bf16[192,512]{1,0:T(8,128)(2,1)} %param.14) | copy-start | bytes 589828
  122.4 3.0 %copy-start.9 = (f32[192,4]{0,1:T(4,128)S(1)}, f32[192,4]{0,1:T(4,128)}, u32[]{:S(2)}) copy-start(f32[192,4]{0,1:T(4,128)} %get-tuple-element.1032) | copy-start | bytes 9220 | tf_op jit(solution)/shard_map/while
  126.9 3.0 %copy-start.9 = (f32[192,4]{0,1:T(4,128)S(1)}, f32[192,4]{0,1:T(4,128)}, u32[]{:S(2)}) copy-start(f32[192,4]{0,1:T(4,128)} %get-tuple-element.1032) | copy-start | bytes 9220 | tf_op jit(solution)/shard_map/while
  131.5 3.0 %copy-start.9 = (f32[192,4]{0,1:T(4,128)S(1)}, f32[192,4]{0,1:T(4,128)}, u32[]{:S(2)}) copy-start(f32[192,4]{0,1:T(4,128)} %get-tuple-element.1032) | copy-start | bytes 9220 | tf_op jit(solution)/shard_map/while
  136.0 3.0 %copy-start.9 = (f32[192,4]{0,1:T(4,128)S(1)}, f32[192,4]{0,1:T(4,128)}, u32[]{:S(2)}) copy-start(f32[192,4]{0,1:T(4,128)} %get-tuple-element.1032) | copy-start | bytes 9220 | tf_op jit(solution)/shard_map/while
  151.6 1.0 copy-start.7
  158.9 1.9 copy-start.7
  167.1 1.9 copy-start.7
  175.3 1.9 copy-start.7
  177.8 2.6 %copy-start.1 = (f32[192,128]{1,0:T(8,128)}, f32[192,128]{1,0:T(8,128)S(1)}, u32[]{:S(2)}) copy-start(f32[192,128]{1,0:T(8,128)S(1)} %get-tuple-element.598) | copy-start | bytes 294916
  177.8 2.6 %copy-start.2 = (f32[192,128]{1,0:T(8,128)S(1)}, f32[192,128]{1,0:T(8,128)}, u32[]{:S(2)}) copy-start(f32[192,128]{1,0:T(8,128)} %get-tuple-element.599) | copy-start | bytes 294916
  177.8 2.6 %copy-start.5 = (bf16[4096,128]{1,0:T(8,128)(2,1)S(1)}, bf16[4096,128]{1,0:T(8,128)(2,1)}, u32[]{:S(2)}) copy-start(bf16[4096,128]{1,0:T(8,128)(2,1)} %param.23) | copy-start | bytes 3145732
Sparse Core Ops, SparseCore 0:
  10.2 50.0 all-gather.4
  62.5 45.3 all-gather.6
  182.8 36.6 reduce-scatter.1
